TPU v7x, 256 devices: a whole 4x4x8 slice. The times are simulated.
256 devices in a mesh: trial: 2 (over core), qa: 16 (over y, x), qb: 8 (over z).
Axes of the slice: x: 4, y: 4, z: 8, core: 2. Of those that a mesh axis runs over, the one named last changes fastest.
Arguments:
- wave_parts: float32 [4, 512, 128, 128], P('trial', ('qa', 'qb')), parts along dimension 0, may hold values from -6 to 6
- level_table: float32 [1024, 128, 128], P(('trial', 'qa', 'qb')), parts along dimension 0, may hold values from -2 to 2
- diagonal_angles: float32 [6, 128], P('trial'), parts along dimension 0, may hold values from 0.3 to 1.2
- turn_angles: float32 [6, 4], P('trial'), parts along dimension 0, may hold values from 0.3 to 1.2
Outputs:
- final_parts: float32 [4, 512, 128, 128], P('trial', ('qa', 'qb')), parts along dimension 0
There are 2 independent parts, one for each index of `trial`. A program takes and returns all parts, laid end to end along the dimension named above; each array names one. Nothing has to cross between parts.
All inputs are finite; a program needn't handle non-finite values.
Results may differ from a plain program's by a relative error of at most 0.0003.
Values sent between devices are 32-bit elements.
A program may use at most 64 MiB of HBM per device.

v0:
```python
import jax
import jax.numpy as jnp
from jax import lax
from jax.sharding import PartitionSpec as P

LAYERS = 3


def count_bits(values, count):
    places = jnp.arange(count.bit_length() - 1, dtype=jnp.int32)
    return jnp.sum(values[..., None] >> places & 1, axis=-1)


def rotation_table(count, angle):
    rank = jnp.arange(count, dtype=jnp.int32)
    apart = count_bits(rank[:, None] ^ rank[None, :], count)
    bits = count.bit_length() - 1
    size = jnp.cos(angle) ** (bits - apart).astype(jnp.float32) * jnp.sin(angle) ** apart.astype(
        jnp.float32
    )
    real_sign = jnp.where(apart % 4 == 0, 1.0, jnp.where(apart % 4 == 2, -1.0, 0.0)).astype(
        jnp.float32
    )
    imag_sign = jnp.where(apart % 4 == 1, -1.0, jnp.where(apart % 4 == 3, 1.0, 0.0)).astype(
        jnp.float32
    )
    return (size * real_sign, size * imag_sign)


def mix_dim(values, dim, angle):
    real_part, imag_part = rotation_table(values.shape[dim], angle)

    def times(table):
        moved = jnp.tensordot(values, table, axes=([dim], [0]), precision=lax.Precision.HIGHEST)
        return jnp.moveaxis(moved, -1, dim)

    by_real = times(real_part)
    by_imag = times(imag_part)
    return jnp.stack([by_real[0] - by_imag[1], by_real[1] + by_imag[0]])


def phase_step(values, levels, angle):
    turn = angle * levels
    return jnp.stack(
        [
            values[0] * jnp.cos(turn) + values[1] * jnp.sin(turn),
            values[1] * jnp.cos(turn) - values[0] * jnp.sin(turn),
        ]
    )


def shards(wave_parts, level_table, diagonal_angles, turn_angles):
    values = wave_parts
    for layer in range(LAYERS):
        values = phase_step(values, level_table, diagonal_angles[layer])
        values = mix_dim(values, 3, turn_angles[layer, 0])
        values = mix_dim(values, 2, turn_angles[layer, 1])
        moved = lax.all_to_all(values, "qa", split_axis=2, concat_axis=1, tiled=True)
        moved = mix_dim(moved, 1, turn_angles[layer, 2])
        values = lax.all_to_all(moved, "qa", split_axis=1, concat_axis=2, tiled=True)
        moved = lax.all_to_all(values, "qb", split_axis=3, concat_axis=1, tiled=True)
        spread = moved.reshape(2, lax.axis_size("qb"), -1, moved.shape[2], moved.shape[3])
        moved = mix_dim(spread, 1, turn_angles[layer, 3]).reshape(moved.shape)
        values = lax.all_to_all(moved, "qb", split_axis=1, concat_axis=3, tiled=True)
    return values


def solution(mesh):
    placed = (
        P("trial", ("qa", "qb"), None, None),
        P(("trial", "qa", "qb"), None, None),
        P("trial", None),
        P("trial", None),
    )
    return jax.shard_map(
        shards,
        mesh=mesh,
        in_specs=placed,
        out_specs=P("trial", ("qa", "qb"), None, None),
        check_vma=False,
    )
```

profile of v0, /device:TPU:32, one launch (start us, length us, event | category | flops | bytes accessed | tf_op | source)
XLA Modules:
  0.0 244.3 jit_solution(5712961371041318198)
XLA Ops:
  0.0 1.8 fusion.327
  3.8 2.0 fusion.19
  9.0 1.1 convolution_bitcast_fusion.17
  10.1 1.1 convolution_bitcast_fusion.16
  11.3 1.0 copy.169
  12.3 7.0 %all-to-all-start = ((f32[2,4,128,128]{3,1,0,2:T(4,128)}), f32[2,4,128,128]{3,1,0,2:T(4,128)S(1)}, u32[]{:S(2)}, u32[]{:S(2)}) async-start(f32[2,4,128,128]{3,1,0,2:T(4,128)} %copy.169), calls=%async_computation | async-start | bytes 1048576 | tf_op jit(solution)/shard_map/all_to_all | solution.py:58
  20.9 10.6 %all-to-all-done = f32[2,4,128,128]{3,1,0,2:T(4,128)S(1)} async-done(((f32[2,4,128,128]{3,1,0,2:T(4,128)}), f32[2,4,128,128]{3,1,0,2:T(4,128)S(1)}, u32[]{:S(2)}, u32[]{:S(2)}) %all-to-all-start) | async-done | bytes 524320 | tf_op jit(solution)/shard_map/all_to_all | solution.py:58
  33.8 13.4 %all_to_all.201 = f32[2,64,8,128]{3,2,0,1:T(8,128)S(1)} all-to-all(f32[2,64,8,128]{3,2,0,1:T(8,128)S(1)} %copy.174), channel_id=1, replica_groups=mesh['trial'=2,'qa'=16,'qb'=8] {'qa'}, dimensions={1} | all-to-all | bytes 1048576 | tf_op jit(solution)/shard_map/all_to_all | solution.py:60
  47.3 1.0 copy.177
  48.3 8.6 %all-to-all-start.2 = ((f32[2,4,128,128]{2,1,0,3:T(4,128)}), f32[2,4,128,128]{2,1,0,3:T(4,128)S(1)}, u32[]{:S(2)}, u32[]{:S(2)}) async-start(f32[2,4,128,128]{2,1,0,3:T(4,128)} %copy.177), calls=%async_computation.2 | async-start | bytes 1048576 | tf_op jit(solution)/shard_map/all_to_all | solution.py:61
  58.4 12.7 %all-to-all-done.2 = f32[2,4,128,128]{2,1,0,3:T(4,128)S(1)} async-done(((f32[2,4,128,128]{2,1,0,3:T(4,128)}), f32[2,4,128,128]{2,1,0,3:T(4,128)S(1)}, u32[]{:S(2)}, u32[]{:S(2)}) %all-to-all-start.2) | async-done | bytes 524320 | tf_op jit(solution)/shard_map/all_to_all | solution.py:61
  73.9 4.7 %all-to-all-start.3 = ((f32[2,32,128,16]{2,3,0,1:T(8,128)}), f32[2,32,128,16]{2,3,0,1:T(8,128)S(1)}, u32[]{:S(2)}, u32[]{:S(2)}) async-start(f32[2,32,128,16]{2,3,0,1:T(8,128)} %copy.184), calls=%async_computation.3 | async-start | bytes 1048576 | tf_op jit(solution)/shard_map/all_to_all | solution.py:64
  81.2 10.7 %all-to-all-done.3 = f32[2,32,128,16]{2,3,0,1:T(8,128)S(1)} async-done(((f32[2,32,128,16]{2,3,0,1:T(8,128)}), f32[2,32,128,16]{2,3,0,1:T(8,128)S(1)}, u32[]{:S(2)}, u32[]{:S(2)}) %all-to-all-start.3) | async-done | bytes 524320 | tf_op jit(solution)/shard_map/all_to_all | solution.py:64
  93.2 1.0 add_bitcast_fusion.1
  95.8 1.1 convolution_bitcast_fusion.11
  96.9 1.1 convolution_bitcast_fusion.10
  99.1 4.9 %all-to-all-start.4 = ((f32[2,4,128,128]{3,1,0,2:T(4,128)}), f32[2,4,128,128]{3,1,0,2:T(4,128)S(1)}, u32[]{:S(2)}, u32[]{:S(2)}) async-start(f32[2,4,128,128]{3,1,0,2:T(4,128)} %copy.194), calls=%async_computation.4 | async-start | bytes 1048576 | tf_op jit(solution)/shard_map/all_to_all | solution.py:58
  105.4 8.7 %all-to-all-done.4 = f32[2,4,128,128]{3,1,0,2:T(4,128)S(1)} async-done(((f32[2,4,128,128]{3,1,0,2:T(4,128)}), f32[2,4,128,128]{3,1,0,2:T(4,128)S(1)}, u32[]{:S(2)}, u32[]{:S(2)}) %all-to-all-start.4) | async-done | bytes 524320 | tf_op jit(solution)/shard_map/all_to_all | solution.py:58
  116.5 12.7 %all_to_all.202 = f32[2,64,8,128]{3,2,0,1:T(8,128)S(1)} all-to-all(f32[2,64,8,128]{3,2,0,1:T(8,128)S(1)} %copy.199), channel_id=1, replica_groups=mesh['trial'=2,'qa'=16,'qb'=8] {'qa'}, dimensions={1} | all-to-all | bytes 1048576 | tf_op jit(solution)/shard_map/all_to_all | solution.py:60
  130.3 5.3 %all-to-all-start.6 = ((f32[2,4,128,128]{2,1,0,3:T(4,128)}), f32[2,4,128,128]{2,1,0,3:T(4,128)S(1)}, u32[]{:S(2)}, u32[]{:S(2)}) async-start(f32[2,4,128,128]{2,1,0,3:T(4,128)} %copy.202), calls=%async_computation.6 | async-start | bytes 1048576 | tf_op jit(solution)/shard_map/all_to_all | solution.py:61
  136.9 12.6 %all-to-all-done.6 = f32[2,4,128,128]{2,1,0,3:T(4,128)S(1)} async-done(((f32[2,4,128,128]{2,1,0,3:T(4,128)}), f32[2,4,128,128]{2,1,0,3:T(4,128)S(1)}, u32[]{:S(2)}, u32[]{:S(2)}) %all-to-all-start.6) | async-done | bytes 524320 | tf_op jit(solution)/shard_map/all_to_all | solution.py:61
  152.4 4.8 %all-to-all-start.7 = ((f32[2,32,128,16]{2,3,0,1:T(8,128)}), f32[2,32,128,16]{2,3,0,1:T(8,128)S(1)}, u32[]{:S(2)}, u32[]{:S(2)}) async-start(f32[2,32,128,16]{2,3,0,1:T(8,128)} %copy.209), calls=%async_computation.7 | async-start | bytes 1048576 | tf_op jit(solution)/shard_map/all_to_all | solution.py:64
  160.1 9.5 %all-to-all-done.7 = f32[2,32,128,16]{2,3,0,1:T(8,128)S(1)} async-done(((f32[2,32,128,16]{2,3,0,1:T(8,128)}), f32[2,32,128,16]{2,3,0,1:T(8,128)S(1)}, u32[]{:S(2)}, u32[]{:S(2)}) %all-to-all-start.7) | async-done | bytes 524320 | tf_op jit(solution)/shard_map/all_to_all | solution.py:64
  170.0 1.0 add_bitcast_fusion
  172.6 1.1 convolution_bitcast_fusion.5
  173.7 1.1 convolution_bitcast_fusion.4
  176.0 6.2 %all-to-all-start.8 = ((f32[2,4,128,128]{3,1,0,2:T(4,128)}), f32[2,4,128,128]{3,1,0,2:T(4,128)S(1)}, u32[]{:S(2)}, u32[]{:S(2)}) async-start(f32[2,4,128,128]{3,1,0,2:T(4,128)} %copy.219), calls=%async_computation.8 | async-start | bytes 1048576 | tf_op jit(solution)/shard_map/all_to_all | solution.py:58
  183.6 8.7 %all-to-all-done.8 = f32[2,4,128,128]{3,1,0,2:T(4,128)S(1)} async-done(((f32[2,4,128,128]{3,1,0,2:T(4,128)}), f32[2,4,128,128]{3,1,0,2:T(4,128)S(1)}, u32[]{:S(2)}, u32[]{:S(2)}) %all-to-all-start.8) | async-done | bytes 524320 | tf_op jit(solution)/shard_map/all_to_all | solution.py:58
  194.6 12.8 %all_to_all.203 = f32[2,64,8,128]{3,2,0,1:T(8,128)S(1)} all-to-all(f32[2,64,8,128]{3,2,0,1:T(8,128)S(1)} %copy.224), channel_id=1, replica_groups=mesh['trial'=2,'qa'=16,'qb'=8] {'qa'}, dimensions={1} | all-to-all | bytes 1048576 | tf_op jit(solution)/shard_map/all_to_all | solution.py:60
  208.4 4.5 %all-to-all-start.10 = ((f32[2,4,128,128]{2,1,0,3:T(4,128)}), f32[2,4,128,128]{2,1,0,3:T(4,128)S(1)}, u32[]{:S(2)}, u32[]{:S(2)}) async-start(f32[2,4,128,128]{2,1,0,3:T(4,128)} %copy.227), calls=%async_computation.10 | async-start | bytes 1048576 | tf_op jit(solution)/shard_map/all_to_all | solution.py:61
  214.4 10.6 %all-to-all-done.10 = f32[2,4,128,128]{2,1,0,3:T(4,128)S(1)} async-done(((f32[2,4,128,128]{2,1,0,3:T(4,128)}), f32[2,4,128,128]{2,1,0,3:T(4,128)S(1)}, u32[]{:S(2)}, u32[]{:S(2)}) %all-to-all-start.10) | async-done | bytes 524320 | tf_op jit(solution)/shard_map/all_to_all | solution.py:61
  227.1 16.2 %all_to_all.204 = f32[2,32,128,16]{2,3,0,1:T(8,128)S(1)} all-to-all(f32[2,32,128,16]{2,3,0,1:T(8,128)S(1)} %copy.234), channel_id=1, replica_groups=mesh['trial'=2,'qa'=16,'qb'=8] {'qb'}, dimensions={1} | all-to-all | bytes 1048576 | tf_op jit(solution)/shard_map/all_to_all | solution.py:64
  (89 shorter events, 27.1 us)
Async XLA Ops:
  3.1 0.7 copy-start.1
  12.3 19.2 %all-to-all-start = ((f32[2,4,128,128]{3,1,0,2:T(4,128)}), f32[2,4,128,128]{3,1,0,2:T(4,128)S(1)}, u32[]{:S(2)}, u32[]{:S(2)}) async-start(f32[2,4,128,128]{3,1,0,2:T(4,128)} %copy.169), calls=%async_computation | async-start | bytes 1048576 | tf_op jit(solution)/shard_map/all_to_all | solution.py:58
  48.3 22.8 %all-to-all-start.2 = ((f32[2,4,128,128]{2,1,0,3:T(4,128)}), f32[2,4,128,128]{2,1,0,3:T(4,128)S(1)}, u32[]{:S(2)}, u32[]{:S(2)}) async-start(f32[2,4,128,128]{2,1,0,3:T(4,128)} %copy.177), calls=%async_computation.2 | async-start | bytes 1048576 | tf_op jit(solution)/shard_map/all_to_all | solution.py:61
  73.9 18.0 %all-to-all-start.3 = ((f32[2,32,128,16]{2,3,0,1:T(8,128)}), f32[2,32,128,16]{2,3,0,1:T(8,128)S(1)}, u32[]{:S(2)}, u32[]{:S(2)}) async-start(f32[2,32,128,16]{2,3,0,1:T(8,128)} %copy.184), calls=%async_computation.3 | async-start | bytes 1048576 | tf_op jit(solution)/shard_map/all_to_all | solution.py:64
  92.2 1.0 copy-start
  99.1 15.0 %all-to-all-start.4 = ((f32[2,4,128,128]{3,1,0,2:T(4,128)}), f32[2,4,128,128]{3,1,0,2:T(4,128)S(1)}, u32[]{:S(2)}, u32[]{:S(2)}) async-start(f32[2,4,128,128]{3,1,0,2:T(4,128)} %copy.194), calls=%async_computation.4 | async-start | bytes 1048576 | tf_op jit(solution)/shard_map/all_to_all | solution.py:58
  130.3 19.3 %all-to-all-start.6 = ((f32[2,4,128,128]{2,1,0,3:T(4,128)}), f32[2,4,128,128]{2,1,0,3:T(4,128)S(1)}, u32[]{:S(2)}, u32[]{:S(2)}) async-start(f32[2,4,128,128]{2,1,0,3:T(4,128)} %copy.202), calls=%async_computation.6 | async-start | bytes 1048576 | tf_op jit(solution)/shard_map/all_to_all | solution.py:61
  152.4 17.2 %all-to-all-start.7 = ((f32[2,32,128,16]{2,3,0,1:T(8,128)}), f32[2,32,128,16]{2,3,0,1:T(8,128)S(1)}, u32[]{:S(2)}, u32[]{:S(2)}) async-start(f32[2,32,128,16]{2,3,0,1:T(8,128)} %copy.209), calls=%async_computation.7 | async-start | bytes 1048576 | tf_op jit(solution)/shard_map/all_to_all | solution.py:64
  176.0 16.3 %all-to-all-start.8 = ((f32[2,4,128,128]{3,1,0,2:T(4,128)}), f32[2,4,128,128]{3,1,0,2:T(4,128)S(1)}, u32[]{:S(2)}, u32[]{:S(2)}) async-start(f32[2,4,128,128]{3,1,0,2:T(4,128)} %copy.219), calls=%async_computation.8 | async-start | bytes 1048576 | tf_op jit(solution)/shard_map/all_to_all | solution.py:58
  208.4 16.6 %all-to-all-start.10 = ((f32[2,4,128,128]{2,1,0,3:T(4,128)}), f32[2,4,128,128]{2,1,0,3:T(4,128)S(1)}, u32[]{:S(2)}, u32[]{:S(2)}) async-start(f32[2,4,128,128]{2,1,0,3:T(4,128)} %copy.227), calls=%async_computation.10 | async-start | bytes 1048576 | tf_op jit(solution)/shard_map/all_to_all | solution.py:61
where the time goes:
time: 246 us; the launch traced here: 244 us
  waiting for transfers between devices  84 us (34%)
  blocking collectives  55.1 us (22%)
  starting transfers between devices  46 us (19%)
  matrix products  20.9 us (8%)
  between operations  17.6 us (7%)
  local copies, waits for them, and re-layouts  15.4 us (6%)
  other arithmetic  5.26 us (2%)
    all_to_all x3, blocking collectives, shards(): lax.all_to_all(moved, 'qa', split_axis=1, concat_axis=2, tiled=True)  38.9 us
    all_to_all x3, waiting for transfers between devices, shards(): lax.all_to_all(values, 'qb', split_axis=3, concat_axis=1, tiled=True)  35.8 us
    all_to_all x3, waiting for transfers between devices, shards(): lax.all_to_all(values, 'qa', split_axis=2, concat_axis=1, tiled=True)  28 us
    dot_general x24, matrix products, times(): jnp.tensordot(values, table, axes=([dim], [0]), precision=lax.Precision.H...  20.9 us
    all_to_all x2, waiting for transfers between devices, shards(): lax.all_to_all(moved, 'qb', split_axis=1, concat_axis=3, tiled=True)  20.2 us
    all_to_all x3, starting transfers between devices, shards(): lax.all_to_all(values, 'qb', split_axis=3, concat_axis=1, tiled=True)  18.5 us
    all_to_all x3, starting transfers between devices, shards(): lax.all_to_all(values, 'qa', split_axis=2, concat_axis=1, tiled=True)  18.1 us
    all_to_all x1, blocking collectives, shards(): lax.all_to_all(moved, 'qb', split_axis=1, concat_axis=3, tiled=True)  16.2 us
  transfers between devices with their start and end apart: 8, of which 8 were waited for; matrix products, arithmetic and copies ran while one was open for 0% of the time, Pallas kernels for 0%

commit v1 on v0

v1 whole, which is shorter than its diff:
```python
import jax
import jax.numpy as jnp
from jax import lax
from jax.experimental import pallas as pl
from jax.experimental.pallas import tpu as pltpu
from jax.sharding import PartitionSpec as P

MESH = pl.DeviceIdType.MESH
N = 128
F32, BF16 = jnp.float32, jnp.bfloat16
NN = (((1,), (0,)), ((), ()))
NT = (((1,), (1,)), ((), ()))
LANE, ROW, QUBITS = (0,) * 7, (1,) * 7, (3, 3, 3, 2, 2, 2, 2)
TABLES = ((0, ROW), (0, LANE), (0, QUBITS), (1, QUBITS), (1, LANE), (1, ROW), (2, ROW), (2, QUBITS), (2, LANE))


def cos_sin(x):
    y = x * 0.5
    z = y * y
    s = z * (-1.0 / 39916800.0) + 1.0 / 362880.0
    for k in (-1.0 / 5040.0, 1.0 / 120.0, -1.0 / 6.0, 1.0):
        s = s * z + k
    c = z * (1.0 / 479001600.0) - 1.0 / 3628800.0
    for k in (1.0 / 40320.0, -1.0 / 720.0, 1.0 / 24.0, -0.5, 1.0):
        c = c * z + k
    s = s * y
    return 1.0 - 2.0 * s * s, 2.0 * s * c


def split(x):
    high = x.astype(BF16)
    return high, (x - high.astype(F32)).astype(BF16)


def dot3(a, b, dims):
    dot = lambda u, v: lax.dot_general(u, v, dims, preferred_element_type=F32)
    return dot(a[0], b[0]) + (dot(a[0], b[1]) + dot(a[1], b[0]))


def strided(part, step):
    return pl.ds(part, N, stride=step)


def kernel(
    wave_hbm, level_hbm, diag_ref, turn_ref, out_ref,
    wave, level, high, low, mixed, cos_ref, sin_ref,
    send_b, send_lb, send_lc, send_c, send_a, got_b, got_lb, got_lc, got_c, got_a,
    load_sem, send_sem, recv_sem,
):
    trial, qa, qb = lax.axis_index("trial"), lax.axis_index("qa"), lax.axis_index("qb")
    me = qa * 8 + qb

    def peer(k):
        p = lax.rem(me + k, N)
        return p, (trial, p // 8, lax.rem(p, 8))

    barrier = pltpu.get_barrier_semaphore()

    @pl.loop(1, N)
    def _(k):
        pl.semaphore_signal(barrier, inc=1, device_id=peer(k)[1], device_id_type=MESH)

    loads = [
        pltpu.make_async_copy(level_hbm, level, load_sem.at[0]),
        pltpu.make_async_copy(wave_hbm, wave, load_sem.at[1]),
    ]
    for load in loads:
        load.start()

    def exchange(slot, source, target, rows):
        @pl.loop(1, N)
        def _(k):
            p, where = peer(k)
            pltpu.make_async_remote_copy(
                source.at[pl.ds(pl.multiple_of(p * rows, rows), rows)],
                target.at[pl.ds(pl.multiple_of(me * rows, rows), rows)],
                send_sem.at[slot],
                recv_sem.at[slot],
                device_id=where,
                device_id_type=MESH,
            ).start()

        own = pl.ds(pl.multiple_of(me * rows, rows), rows)
        target[own, :] = source[own, :]

    def arrive(slot, target, rows):
        span = target.at[pl.ds(0, (N - 1) * rows)]
        pltpu.make_async_copy(span, span, recv_sem.at[slot]).wait()

    def sent(slot, source, rows):
        span = source.at[pl.ds(0, (N - 1) * rows)]
        pltpu.make_async_copy(span, span, send_sem.at[slot]).wait()

    row_i = lax.broadcasted_iota(jnp.int32, (N, N), 0)
    col_i = lax.broadcasted_iota(jnp.int32, (N, N), 1)

    def build(index):
        layer, groups = TABLES[index]
        pairs = {g: cos_sin(jnp.full((1, N), turn_ref[layer, g], F32)) for g in sorted(set(groups))}
        total = None
        for place, g in enumerate(groups):
            c, s = pairs[g]
            own, other = (row_i >> place) & 1, (col_i >> place) & 1
            term = jnp.where(own == other, c, jnp.where(own == 1, s, -s))
            total = term if total is None else total * term
        high[index], low[index] = split(total)

    def table(index):
        return high[index], low[index]

    def mix_blocks(layer, source):
        c, s = cos_sin(jnp.full((1, N), turn_ref[layer, 2], F32))

        @pl.loop(0, 2)
        def _(part):
            u = [source[strided(part * 4 + block, 8), :] for block in range(4)]
            for i, j in ((0, 1), (2, 3), (0, 2), (1, 3)):
                u[i], u[j] = c * u[i] - s * u[j], s * u[i] + c * u[j]
            for block in range(4):
                mixed[part * 4 + block] = u[block]

    build(0)
    build(1)
    loads[0].wait()
    for block in range(4):
        send_lb[strided(block, 4), :] = level[block]
        send_lc[strided(block, 4), :] = level[block].T
    loads[1].wait()

    ones = jnp.zeros((N, N), jnp.int32)
    for place in range(7):
        ones = ones + ((row_i >> place) & 1) + ((col_i >> place) & 1)
    mine = 0
    for place in range(7):
        mine = mine + lax.rem(me // (1 << place), 2)

    @pl.loop(0, 4)
    def _(block):
        c, s = cos_sin(diag_ref[0:1, :] * level[block])
        m = (ones + (mine + block // 2 + lax.rem(block, 2))) & 3
        odd, sign = (m & 1) == 1, jnp.where(m >= 2, -1.0, 1.0)
        real, imag = sign * jnp.where(odd, s, c), sign * jnp.where(odd, c, -s)
        u, v = wave[0, block], wave[1, block]
        both = jnp.concatenate([u * real - v * imag, u * imag + v * real], axis=1)
        both = dot3(table(0), split(both), NN)
        both = jnp.concatenate([both[:, :N], both[:, N:]], axis=0)
        both = dot3(split(both), table(1), NT)
        send_b[strided(block, 8), :] = both[:N]
        send_b[strided(block + 4, 8), :] = both[N:]

    pl.semaphore_wait(barrier, N - 1)
    exchange(0, send_lb, got_lb, 4)
    exchange(1, send_b, got_b, 8)
    exchange(2, send_lc, got_lc, 4)

    def stage(layer, got, slot, first, angle, sending, levels):
        arrive(slot, got, 8)
        mix_blocks(layer, got)

        @pl.loop(0, 4)
        def _(block):
            both = jnp.concatenate([mixed[block], mixed[block + 4]], axis=1)
            both = dot3(table(first), split(both), NN)
            c, s = cos_ref[block], sin_ref[block]
            u, v = both[:, :N], both[:, N:]
            both = jnp.concatenate([u * c + v * s, v * c - u * s], axis=1)
            both = dot3(table(first + 1), split(both), NN)
            sending[strided(block, 8), :] = dot3(table(first + 2), split(both[:, :N]), NT)
            sending[strided(block + 4, 8), :] = dot3(table(first + 2), split(both[:, N:]), NT)

    for index in range(2, 9):
        build(index)
    arrive(0, got_lb, 4)

    @pl.loop(0, 4)
    def _(block):
        cos_ref[block], sin_ref[block] = cos_sin(diag_ref[1:2, :] * got_lb[strided(block, 4), :])

    stage(0, got_b, 1, 2, None, send_c, None)
    exchange(3, send_c, got_c, 8)

    angle = jnp.sum(jnp.where(col_i[0:1] == me, diag_ref[2:3, :], 0.0), axis=1, keepdims=True)
    arrive(2, got_lc, 4)

    @pl.loop(0, 4)
    def _(block):
        cos_ref[block], sin_ref[block] = cos_sin(angle * got_lc[strided(block, 4), :].T)

    stage(1, got_c, 3, 5, None, send_a, None)
    exchange(4, send_a, got_a, 8)

    arrive(4, got_a, 8)
    mix_blocks(2, got_a)

    @pl.loop(0, 4)
    def _(block):
        both = jnp.concatenate([mixed[block], mixed[block + 4]], axis=1)
        both = dot3(table(8), split(both), NN)
        u, v = both[:, :N].T, both[:, N:].T
        m = (4 - ((ones + (mine + block // 2 + lax.rem(block, 2))) & 3)) & 3
        odd, sign = (m & 1) == 1, jnp.where(m >= 2, -1.0, 1.0)
        out_ref[0, block] = sign * jnp.where(odd, -v, u)
        out_ref[1, block] = sign * jnp.where(odd, u, v)

    for slot, source, rows in ((0, send_lb, 4), (1, send_b, 8), (2, send_lc, 4), (3, send_c, 8), (4, send_a, 8)):
        sent(slot, source, rows)


def shards(wave_parts, level_table, diagonal_angles, turn_angles):
    wide, half = pltpu.VMEM((N * 8, N), F32), pltpu.VMEM((N * 4, N), F32)
    return pl.pallas_call(
        kernel,
        out_shape=jax.ShapeDtypeStruct((2, 4, N, N), F32),
        in_specs=[
            pl.BlockSpec(memory_space=pl.ANY),
            pl.BlockSpec(memory_space=pl.ANY),
            pl.BlockSpec(memory_space=pltpu.VMEM),
            pl.BlockSpec(memory_space=pltpu.SMEM),
        ],
        out_specs=pl.BlockSpec(memory_space=pltpu.VMEM),
        scratch_shapes=[
            pltpu.VMEM((2, 4, N, N), F32),
            pltpu.VMEM((4, N, N), F32),
            pltpu.VMEM((9, N, N), BF16),
            pltpu.VMEM((9, N, N), BF16),
            pltpu.VMEM((8, N, N), F32),
            pltpu.VMEM((4, N, N), F32),
            pltpu.VMEM((4, N, N), F32),
            wide, half, half, wide, wide,
            wide, half, half, wide, wide,
            pltpu.SemaphoreType.DMA((2,)),
            pltpu.SemaphoreType.DMA((5,)),
            pltpu.SemaphoreType.DMA((5,)),
        ],
        compiler_params=pltpu.CompilerParams(collective_id=0, has_side_effects=True),
        name="layers",
    )(wave_parts, level_table, diagonal_angles, turn_angles)


def solution(mesh):
    wave = P("trial", ("qa", "qb"), None, None)
    return jax.shard_map(
        shards,
        mesh=mesh,
        in_specs=(wave, P(("trial", "qa", "qb"), None, None), P("trial", None), P("trial", None)),
        out_specs=wave,
        check_vma=False,
    )
```

time: 246 us -> 71.6 us (0.29)
  waiting for transfers between devices: 84 us -> 0 us
  Pallas kernels: 0 us -> 69.6 us
  blocking collectives: 55.1 us -> 0 us
  starting transfers between devices: 46 us -> 0 us
  matrix products: 20.9 us -> 0 us
  between operations: 17.6 us -> 0.01 us
  local copies, waits for them, and re-layouts: 15.4 us -> 1.87 us
  other arithmetic: 5.26 us -> 0 us
    all_to_all x8 -> x0, waiting for transfers between devices: 84 us -> none  [the longest x3 35.8 us: shards(): lax.all_to_all(values, 'qb', split_axis=3, concat_axis=1, tiled=True)]
    pallas_call x0 -> x1, Pallas kernels: none -> 69.6 us  [shards(): pl.pallas_call(kernel, out_shape=jax.ShapeDtypeStruct((2, 4, N, N), F32),...]
    all_to_all x4 -> x0, blocking collectives: 55.1 us -> none  [the longest x3 38.9 us: shards(): lax.all_to_all(moved, 'qa', split_axis=1, concat_axis=2, tiled=True)]
    all_to_all x8 -> x0, starting transfers between devices: 46 us -> none  [the longest x3 18.5 us: shards(): lax.all_to_all(values, 'qb', split_axis=3, concat_axis=1, tiled=True)]
    dot_general x24 -> x0, matrix products: 20.9 us -> none  [times(): jnp.tensordot(values, table, axes=([dim], [0]), precision=lax.Precision.H...]
    another operation x9 -> x0, local copies, waits for them, and re-layouts: 5.69 us -> none  [mix_dim(): return jnp.stack([by_real[0] - by_imag[1], by_real[1] + by_imag[0]])]
    all_to_all x16 -> x0, local copies, waits for them, and re-layouts: 5.52 us -> none  [the longest x6 3.09 us: shards(): lax.all_to_all(moved, 'qa', split_axis=1, concat_axis=2, tiled=True)]
    another operation x12 -> x0, other arithmetic: 4.42 us -> none  [the longest x3 4.08 us: phase_step(): jnp.stack([values[0] * jnp.cos(turn) + values[1] * jnp.sin(turn), values[...]
  transfers between devices with their start and end apart: 8 -> 0, of which waited for: 8 -> 0; matrix products, arithmetic and copies ran while one was open for 0% -> 0% of each run, Pallas kernels for 0% -> 0%
where the time goes in v1:
time: 71.6 us; the launch traced here: 71.4 us
  Pallas kernels  69.6 us (97%)
  local copies, waits for them, and re-layouts  1.87 us (3%)
    pallas_call x1, Pallas kernels, shards(): pl.pallas_call(kernel, out_shape=jax.ShapeDtypeStruct((2, 4, N, N), F32),...  69.6 us
    unnamed x1, local copies, waits for them, and re-layouts  1.87 us

profile of v1, /device:TPU:32, one launch (start us, length us, event | category | flops | bytes accessed | tf_op | source)
XLA Modules:
  0.0 71.4 jit_solution(4721979889454156503)
XLA Ops:
  0.0 69.6 %layers.1 = f32[2,4,128,128]{3,2,1,0:T(8,128)} custom-call(f32[2,4,128,128]{3,2,1,0:T(8,128)} %wave_hbm.1, f32[4,128,128]{2,1,0:T(8,128)} %level_hbm.1, f32[3,128]{1,0:T(4,128)} %diag_ref.1, f32[3,4]{1,0:T(4,128)} %turn_ref.1), custom_call_target="tpu_custom_call" | custom-call | tf_op jit(solution)/shard_map/layers/pallas_call | solution.py:211
  69.6 1.9 %copy.6 = f32[2,4,128,128]{3,2,1,0:T(8,128)} copy(f32[2,4,128,128]{3,2,1,0:T(8,128)} %layers.1) | data formatting | bytes 1048576

commit v2 on v1

--- a/solution.py
+++ b/solution.py
@@ -50,15 +50,24 @@
     trial, qa, qb = lax.axis_index("trial"), lax.axis_index("qa"), lax.axis_index("qb")
     me = qa * 8 + qb
 
-    def peer(k):
-        p = lax.rem(me + k, N)
-        return p, (trial, p // 8, lax.rem(p, 8))
-
     barrier = pltpu.get_barrier_semaphore()
 
-    @pl.loop(1, N)
-    def _(k):
-        pl.semaphore_signal(barrier, inc=1, device_id=peer(k)[1], device_id_type=MESH)
+    def others(visit):
+        @pl.loop(0, 16)
+        def _(u):
+            y = lax.rem(qa // 4 + 2 + 3 * (u // 4), 4)
+            x = lax.rem(qa + 2 + 3 * u, 4)
+            for step in (4, 3, 5, 2, 6, 1, 7):
+                visit((y * 4 + x) * 8 + lax.rem(qb + step, 8))
+
+        @pl.loop(0, 5)
+        def _(u):
+            for k in (1, 2, 3):
+                visit(lax.rem(qa + u * 3 + k, 16) * 8 + qb)
+
+    @others
+    def _(p):
+        pl.semaphore_signal(barrier, inc=1, device_id=(trial, lax.div(p, 8), lax.rem(p, 8)), device_id_type=MESH)
 
     loads = [
         pltpu.make_async_copy(level_hbm, level, load_sem.at[0]),
@@ -68,19 +77,19 @@
         load.start()
 
     def exchange(slot, source, target, rows):
-        @pl.loop(1, N)
-        def _(k):
-            p, where = peer(k)
+        own = pl.ds(pl.multiple_of(me * rows, rows), rows)
+
+        @others
+        def _(p):
             pltpu.make_async_remote_copy(
                 source.at[pl.ds(pl.multiple_of(p * rows, rows), rows)],
-                target.at[pl.ds(pl.multiple_of(me * rows, rows), rows)],
+                target.at[own],
                 send_sem.at[slot],
                 recv_sem.at[slot],
-                device_id=where,
+                device_id=(trial, lax.div(p, 8), lax.rem(p, 8)),
                 device_id_type=MESH,
             ).start()
 
-        own = pl.ds(pl.multiple_of(me * rows, rows), rows)
         target[own, :] = source[own, :]
 
     def arrive(slot, target, rows):
@@ -111,7 +120,7 @@
     def mix_blocks(layer, source):
         c, s = cos_sin(jnp.full((1, N), turn_ref[layer, 2], F32))
 
-        @pl.loop(0, 2)
+        @pl.loop(0, 2, unroll=2)
         def _(part):
             u = [source[strided(part * 4 + block, 8), :] for block in range(4)]
             for i, j in ((0, 1), (2, 3), (0, 2), (1, 3)):
@@ -134,7 +143,7 @@
     for place in range(7):
         mine = mine + lax.rem(me // (1 << place), 2)
 
-    @pl.loop(0, 4)
+    @pl.loop(0, 4, unroll=4)
     def _(block):
         c, s = cos_sin(diag_ref[0:1, :] * level[block])
         m = (ones + (mine + block // 2 + lax.rem(block, 2))) & 3
@@ -153,11 +162,11 @@
     exchange(1, send_b, got_b, 8)
     exchange(2, send_lc, got_lc, 4)
 
-    def stage(layer, got, slot, first, angle, sending, levels):
+    def stage(layer, got, slot, first, sending):
         arrive(slot, got, 8)
         mix_blocks(layer, got)
 
-        @pl.loop(0, 4)
+        @pl.loop(0, 4, unroll=4)
         def _(block):
             both = jnp.concatenate([mixed[block], mixed[block + 4]], axis=1)
             both = dot3(table(first), split(both), NN)
@@ -172,27 +181,27 @@
         build(index)
     arrive(0, got_lb, 4)
 
-    @pl.loop(0, 4)
+    @pl.loop(0, 4, unroll=4)
     def _(block):
         cos_ref[block], sin_ref[block] = cos_sin(diag_ref[1:2, :] * got_lb[strided(block, 4), :])
 
-    stage(0, got_b, 1, 2, None, send_c, None)
+    stage(0, got_b, 1, 2, send_c)
     exchange(3, send_c, got_c, 8)
 
     angle = jnp.sum(jnp.where(col_i[0:1] == me, diag_ref[2:3, :], 0.0), axis=1, keepdims=True)
     arrive(2, got_lc, 4)
 
-    @pl.loop(0, 4)
+    @pl.loop(0, 4, unroll=4)
     def _(block):
         cos_ref[block], sin_ref[block] = cos_sin(angle * got_lc[strided(block, 4), :].T)
 
-    stage(1, got_c, 3, 5, None, send_a, None)
+    stage(1, got_c, 3, 5, send_a)
     exchange(4, send_a, got_a, 8)
 
     arrive(4, got_a, 8)
     mix_blocks(2, got_a)
 
-    @pl.loop(0, 4)
+    @pl.loop(0, 4, unroll=4)
     def _(block):
         both = jnp.concatenate([mixed[block], mixed[block + 4]], axis=1)
         both = dot3(table(8), split(both), NN)

time: 71.6 us -> 71.5 us (level); the launches traced: 71.4 us -> 70.4 us
  Pallas kernels: 69.6 us -> 68.5 us
    pallas_call x1, Pallas kernels: 69.6 us -> 68.5 us  [shards(): pl.pallas_call(kernel, out_shape=jax.ShapeDtypeStruct((2, 4, N, N), F32),...]
where the time goes in v2:
time: 71.5 us; the launch traced here: 70.4 us
  Pallas kernels  68.5 us (96%)
  local copies, waits for them, and re-layouts  1.87 us (3%)
    pallas_call x1, Pallas kernels, shards(): pl.pallas_call(kernel, out_shape=jax.ShapeDtypeStruct((2, 4, N, N), F32),...  68.5 us
    unnamed x1, local copies, waits for them, and re-layouts  1.87 us

profile of v2, /device:TPU:32, one launch (start us, length us, event | category | flops | bytes accessed | tf_op | source)
XLA Modules:
  0.0 70.4 jit_solution(12386833540922240556)
XLA Ops:
  0.0 68.5 %layers.1 = f32[2,4,128,128]{3,2,1,0:T(8,128)} custom-call(f32[2,4,128,128]{3,2,1,0:T(8,128)} %wave_hbm.1, f32[4,128,128]{2,1,0:T(8,128)} %level_hbm.1, f32[3,128]{1,0:T(4,128)} %diag_ref.1, f32[3,4]{1,0:T(4,128)} %turn_ref.1), custom_call_target="tpu_custom_call" | custom-call | tf_op jit(solution)/shard_map/layers/pallas_call | solution.py:220
  68.5 1.9 %copy.6 = f32[2,4,128,128]{3,2,1,0:T(8,128)} copy(f32[2,4,128,128]{3,2,1,0:T(8,128)} %layers.1) | data formatting | bytes 1048576

commit v3 on v2

--- a/solution.py
+++ b/solution.py
@@ -43,10 +43,11 @@
 
 def kernel(
     wave_hbm, level_hbm, diag_ref, turn_ref, out_ref,
-    wave, level, high, low, mixed, cos_ref, sin_ref,
-    send_b, send_lb, send_lc, send_c, send_a, got_b, got_lb, got_lc, got_c, got_a,
+    wave, level, high, low, mixed, turned, cos_ref, sin_ref,
+    send_b, got_b, send_lb, send_lc, got_lb, got_lc, send_c0, send_c1, got_c0, got_c1, send_a0, send_a1, got_a0, got_a1,
     load_sem, send_sem, recv_sem,
 ):
+    send_c, got_c, send_a, got_a = (send_c0, send_c1), (got_c0, got_c1), (send_a0, send_a1), (got_a0, got_a1)
     trial, qa, qb = lax.axis_index("trial"), lax.axis_index("qa"), lax.axis_index("qb")
     me = qa * 8 + qb
 
@@ -117,16 +118,19 @@
     def table(index):
         return high[index], low[index]
 
-    def mix_blocks(layer, source):
+    def mix_blocks(layer, source, target=None):
         c, s = cos_sin(jnp.full((1, N), turn_ref[layer, 2], F32))
 
-        @pl.loop(0, 2, unroll=2)
+        @pl.loop(0, 2)
         def _(part):
-            u = [source[strided(part * 4 + block, 8), :] for block in range(4)]
+            u = [source(block, part) for block in range(4)]
             for i, j in ((0, 1), (2, 3), (0, 2), (1, 3)):
                 u[i], u[j] = c * u[i] - s * u[j], s * u[i] + c * u[j]
             for block in range(4):
-                mixed[part * 4 + block] = u[block]
+                if target is None:
+                    mixed[block * 2 + part] = u[block]
+                else:
+                    target[block // 2][strided(block % 2 * 2 + part, 4), :] = u[block]
 
     build(0)
     build(1)
@@ -143,7 +147,7 @@
     for place in range(7):
         mine = mine + lax.rem(me // (1 << place), 2)
 
-    @pl.loop(0, 4, unroll=4)
+    @pl.loop(0, 4)
     def _(block):
         c, s = cos_sin(diag_ref[0:1, :] * level[block])
         m = (ones + (mine + block // 2 + lax.rem(block, 2))) & 3
@@ -154,56 +158,72 @@
         both = dot3(table(0), split(both), NN)
         both = jnp.concatenate([both[:, :N], both[:, N:]], axis=0)
         both = dot3(split(both), table(1), NT)
-        send_b[strided(block, 8), :] = both[:N]
-        send_b[strided(block + 4, 8), :] = both[N:]
+        send_b[strided(block * 2, 8), :] = both[:N]
+        send_b[strided(block * 2 + 1, 8), :] = both[N:]
 
     pl.semaphore_wait(barrier, N - 1)
     exchange(0, send_lb, got_lb, 4)
     exchange(1, send_b, got_b, 8)
     exchange(2, send_lc, got_lc, 4)
 
-    def stage(layer, got, slot, first, sending):
-        arrive(slot, got, 8)
-        mix_blocks(layer, got)
-
-        @pl.loop(0, 4, unroll=4)
-        def _(block):
-            both = jnp.concatenate([mixed[block], mixed[block + 4]], axis=1)
-            both = dot3(table(first), split(both), NN)
-            c, s = cos_ref[block], sin_ref[block]
-            u, v = both[:, :N], both[:, N:]
-            both = jnp.concatenate([u * c + v * s, v * c - u * s], axis=1)
-            both = dot3(table(first + 1), split(both), NN)
-            sending[strided(block, 8), :] = dot3(table(first + 2), split(both[:, :N]), NT)
-            sending[strided(block + 4, 8), :] = dot3(table(first + 2), split(both[:, N:]), NT)
+    def turn(block, first, sources, keep):
+        both = jnp.concatenate(sources, axis=1)
+        both = dot3(table(first), split(both), NN)
+        c, s = cos_ref[block], sin_ref[block]
+        u, v = both[:, :N], both[:, N:]
+        both = jnp.concatenate([u * c + v * s, v * c - u * s], axis=1)
+        both = dot3(table(first + 1), split(both), NN)
+        for part in range(2):
+            keep(part, dot3(table(first + 2), split(both[:, part * N : part * N + N]), NT))
 
     for index in range(2, 9):
         build(index)
     arrive(0, got_lb, 4)
 
+    @pl.loop(0, 4)
+    def _(block):
+        cos_ref[block], sin_ref[block] = cos_sin(diag_ref[1:2, :] * got_lb[strided(block, 4), :])
+
+    arrive(1, got_b, 8)
+    mix_blocks(0, lambda block, part: got_b[strided(block * 2 + part, 8), :])
+
     @pl.loop(0, 4, unroll=4)
     def _(block):
-        cos_ref[block], sin_ref[block] = cos_sin(diag_ref[1:2, :] * got_lb[strided(block, 4), :])
-
-    stage(0, got_b, 1, 2, send_c)
-    exchange(3, send_c, got_c, 8)
+        def keep(part, value):
+            turned[block * 2 + part] = value
+
+        turn(block, 2, [mixed[block * 2], mixed[block * 2 + 1]], keep)
+
+    mix_blocks(1, lambda block, part: turned[block * 2 + part], send_c)
+    exchange(3, send_c[0], got_c[0], 4)
+    exchange(5, send_c[1], got_c[1], 4)
 
     angle = jnp.sum(jnp.where(col_i[0:1] == me, diag_ref[2:3, :], 0.0), axis=1, keepdims=True)
     arrive(2, got_lc, 4)
 
+    @pl.loop(0, 4)
+    def _(block):
+        cos_ref[block], sin_ref[block] = cos_sin(angle * got_lc[strided(block, 4), :].T)
+
+    for half, (came, goes) in enumerate(((3, 4), (5, 6))):
+        arrive(came, got_c[half], 4)
+
+        @pl.loop(0, 2)
+        def _(block):
+            def keep(part, value):
+                send_a[half][strided(block * 2 + part, 4), :] = value
+
+            turn(half * 2 + block, 5, [got_c[half][strided(block * 2 + part, 4), :] for part in range(2)], keep)
+
+        exchange(goes, send_a[half], got_a[half], 4)
+
+    arrive(4, got_a[0], 4)
+    arrive(6, got_a[1], 4)
+    mix_blocks(2, lambda block, part: got_a[block // 2][strided(block % 2 * 2 + part, 4), :])
+
     @pl.loop(0, 4, unroll=4)
     def _(block):
-        cos_ref[block], sin_ref[block] = cos_sin(angle * got_lc[strided(block, 4), :].T)
-
-    stage(1, got_c, 3, 5, send_a)
-    exchange(4, send_a, got_a, 8)
-
-    arrive(4, got_a, 8)
-    mix_blocks(2, got_a)
-
-    @pl.loop(0, 4, unroll=4)
-    def _(block):
-        both = jnp.concatenate([mixed[block], mixed[block + 4]], axis=1)
+        both = jnp.concatenate([mixed[block * 2], mixed[block * 2 + 1]], axis=1)
         both = dot3(table(8), split(both), NN)
         u, v = both[:, :N].T, both[:, N:].T
         m = (4 - ((ones + (mine + block // 2 + lax.rem(block, 2))) & 3)) & 3
@@ -211,7 +231,9 @@
         out_ref[0, block] = sign * jnp.where(odd, -v, u)
         out_ref[1, block] = sign * jnp.where(odd, u, v)
 
-    for slot, source, rows in ((0, send_lb, 4), (1, send_b, 8), (2, send_lc, 4), (3, send_c, 8), (4, send_a, 8)):
+    for slot, source, rows in (
+        (0, send_lb, 4), (1, send_b, 8), (2, send_lc, 4), (3, send_c[0], 4), (5, send_c[1], 4), (4, send_a[0], 4), (6, send_a[1], 4)
+    ):
         sent(slot, source, rows)
 
 
@@ -233,13 +255,13 @@
             pltpu.VMEM((9, N, N), BF16),
             pltpu.VMEM((9, N, N), BF16),
             pltpu.VMEM((8, N, N), F32),
+            pltpu.VMEM((8, N, N), F32),
             pltpu.VMEM((4, N, N), F32),
             pltpu.VMEM((4, N, N), F32),
-            wide, half, half, wide, wide,
-            wide, half, half, wide, wide,
+            wide, wide, *[half] * 12,
             pltpu.SemaphoreType.DMA((2,)),
-            pltpu.SemaphoreType.DMA((5,)),
-            pltpu.SemaphoreType.DMA((5,)),
+            pltpu.SemaphoreType.DMA((7,)),
+            pltpu.SemaphoreType.DMA((7,)),
         ],
         compiler_params=pltpu.CompilerParams(collective_id=0, has_side_effects=True),
         name="layers",

time: 71.5 us -> 67.3 us (0.941)
  Pallas kernels: 68.5 us -> 64.3 us
    pallas_call x1, Pallas kernels: 68.5 us -> 64.3 us  [shards(): pl.pallas_call(kernel, out_shape=jax.ShapeDtypeStruct((2, 4, N, N), F32),...]
where the time goes in v3:
time: 67.3 us; the launch traced here: 66.2 us
  Pallas kernels  64.3 us (96%)
  local copies, waits for them, and re-layouts  1.87 us (3%)
    pallas_call x1, Pallas kernels, shards(): pl.pallas_call(kernel, out_shape=jax.ShapeDtypeStruct((2, 4, N, N), F32),...  64.3 us
    unnamed x1, local copies, waits for them, and re-layouts  1.87 us

profile of v3, /device:TPU:32, one launch (start us, length us, event | category | flops | bytes accessed | tf_op | source)
XLA Modules:
  0.0 66.2 jit_solution(650209648332564184)
XLA Ops:
  0.0 64.3 %layers.1 = f32[2,4,128,128]{3,2,1,0:T(8,128)} custom-call(f32[2,4,128,128]{3,2,1,0:T(8,128)} %wave_hbm.1, f32[4,128,128]{2,1,0:T(8,128)} %level_hbm.1, f32[3,128]{1,0:T(4,128)} %diag_ref.1, f32[3,4]{1,0:T(4,128)} %turn_ref.1), custom_call_target="tpu_custom_call" | custom-call | tf_op jit(solution)/shard_map/layers/pallas_call | solution.py:242
  64.3 1.9 %copy.6 = f32[2,4,128,128]{3,2,1,0:T(8,128)} copy(f32[2,4,128,128]{3,2,1,0:T(8,128)} %layers.1) | data formatting | bytes 1048576
